TPU v7x, 256 devices: a whole 4x4x8 slice. The times are simulated.
256 devices in a mesh: blk: 16 (over x, z_hi), slab: 16 (over y, z_lo, core).
Axes of the slice: x: 4, y: 4, z: 8 (z_hi: 4, z_lo: 2; z = z_hi * 2 + z_lo), core: 2. Of those that a mesh axis runs over, the one named last changes fastest.
Arguments:
- xinv: bfloat16 [16, 4096, 4096], P('blk', None, 'slab'), may hold values from -1 to 16
- ymat: bfloat16 [16, 4096, 4096], P('blk', None, 'slab'), may hold values from -1 to 16
- basis: bfloat16 [16, 4096, 1024], P('blk', 'slab'), may hold values from -0.08118988 to 0.08118988
- pair_index: int32 [16, 2, 512], P('blk'), may hold values from 0 to 1023
- orders: int32 [16], replicated, may hold values from 1 to 512, 4096 in all
- dest: int32 [16], replicated, may hold values from 0 to 15, each once
Outputs:
- factor: float32 [16, 512, 512], P('blk', 'slab')
Inputs may be any that keep to these rules, and one draw needn't show every extreme that they name: `pair_index`: entries name columns of the block's basis. Sum of all orders is 4096; the largest equals 512. `dest`: every group receives exactly one block.
All inputs are finite; a program needn't handle non-finite values.
Results may differ from a plain program's by a relative error of at most 0.0003.
Values may be sent and summed in bfloat16 or wider, within the bound.
A program may use at most 64 MiB of HBM per device.

v0:
```python
import jax
import jax.numpy as jnp
from jax import lax
from jax.sharding import PartitionSpec as P


def cut_along(value, dim, length):
    before, after = (value.shape[:dim], value.shape[dim + 1 :])
    return jnp.moveaxis(value.reshape(*before, length, -1, *after), dim, 0)


def sum_at_owner(value, axis, dim):
    parts = cut_along(value, dim, lax.axis_size(axis))
    arrived = lax.all_to_all(parts, axis, split_axis=0, concat_axis=0, tiled=True)
    return arrived.sum(axis=0)


def from_everyone(value, axis):
    copies = jnp.broadcast_to(value, (lax.axis_size(axis), *value.shape))
    return lax.all_to_all(copies, axis, split_axis=0, concat_axis=0, tiled=True)


def in_order(parts, dim):
    parts = jnp.moveaxis(parts, 0, dim)
    lengths = parts.shape
    return parts.reshape(*lengths[:dim], lengths[dim] * lengths[dim + 1], *lengths[dim + 2 :])


def gathered_copies(value, axis, dim):
    parts = from_everyone(value, axis)
    return in_order(parts, dim)


def add_piece(piece, columns):
    return lax.dot_general(
        piece, columns, (((0,), (0,)), ((), ())), preferred_element_type=jnp.float32
    )


def on_device(xinv, ymat, basis, pair_index, orders, dest):
    xlocal = xinv[0]
    ylocal = ymat[0]
    vlocal = basis[0]
    piece = lax.all_gather(vlocal, "slab", axis=0, tiled=True)
    cx = add_piece(piece, xlocal)
    cy = add_piece(piece, ylocal)
    cx = cx.astype(jnp.bfloat16)
    cy = cy.astype(jnp.bfloat16)
    first = pair_index[0, 0]
    second = pair_index[0, 1]
    order_most = first.shape[0]
    share = order_most // lax.axis_size("slab")
    row_start = lax.axis_index("slab") * share
    basis_first = jnp.take(vlocal, first, axis=1)
    basis_second = jnp.take(vlocal, second, axis=1)
    cx_first = jnp.take(cx, first, axis=0)
    cy_second = jnp.take(cy, second, axis=0)
    stacked = sum_at_owner(
        jnp.concatenate(
            [
                jnp.dot(cx_first, basis_first, preferred_element_type=jnp.float32),
                jnp.dot(cy_second, basis_second, preferred_element_type=jnp.float32),
            ],
            axis=1,
        ),
        "slab",
        0,
    )
    a_ff = stacked[:, :order_most]
    b_ss = stacked[:, order_most:]
    schur = a_ff * b_ss
    block_id = lax.axis_index("blk")
    order = orders[block_id]
    row_ids = row_start + jnp.arange(share, dtype=jnp.int32)
    col_ids = jnp.arange(order_most, dtype=jnp.int32)
    mask = (row_ids[:, None] < order) & (col_ids[None, :] < order)
    diagonal = (row_ids[:, None] == col_ids[None, :]).astype(jnp.float32)
    schur_rows = jnp.where(mask, schur, 0.0) + diagonal
    everyone = gathered_copies(schur_rows, "blk", 0)
    groups = dest.shape[0]
    everyone = everyone.reshape(groups, share, order_most)
    chosen = (dest == block_id).astype(jnp.float32)
    mine = jnp.sum(chosen[:, None, None] * everyone, axis=0)
    whole = gathered_copies(mine, "slab", 0)
    lower = jnp.linalg.cholesky(whole)
    own = lax.dynamic_slice_in_dim(lower, row_start, share, 0)
    return own[None]


def solution(mesh):
    return jax.shard_map(
        on_device,
        mesh=mesh,
        in_specs=(
            P("blk", None, "slab"),
            P("blk", None, "slab"),
            P("blk", "slab", None),
            P("blk", None, None),
            P(),
            P(),
        ),
        out_specs=P("blk", "slab", None),
        check_vma=False,
    )
```

profile of v0, /device:TPU:1, one launch (start us, length us, event | category | flops | bytes accessed | tf_op | source)
XLA Modules:
  0.0 283.8 jit_solution(7355366731148311306)
XLA Ops:
  6.5 0.7 all-gather.3.cloned.1.call-update
  7.3 1.2 copy.12
  8.5 0.8 fusion.46
  9.3 2.0 gather_fusion.1
  11.3 2.0 gather_fusion.3
  13.3 54.8 %all-gather.3.cloned.1.call-done = bf16[1,4096,1024]{2,1,0:T(8,128)(2,1)} async-done(((bf16[1,256,1024]{2,1,0:T(8,128)(2,1)}), bf16[1,4096,1024]{2,1,0:T(8,128)(2,1)}) %all-gather.3.cloned.1.call-update) | async-done | bytes 8388624 | tf_op jit(solution)/shard_map/all_gather | solution.py:44
  68.1 5.8 %fusion.6 = bf16[1024,256]{1,0:T(8,128)(2,1)S(1)} fusion(bf16[1,4096,256]{2,1,0:T(8,128)(2,1)S(1)} %copy-done, bf16[1,4096,1024]{2,1,0:T(8,128)(2,1)} %all-gather.3.cloned.1.call-done), kind=kOutput, calls=%fused_computation.11 | convolution fusion | flops 2147745792 | bytes 11010048 | tf_op jit(solution)/shard_map/dot_general | solution.py:35
  73.8 2.0 gather_fusion
  75.8 6.3 %fusion.11 = bf16[1024,256]{1,0:T(8,128)(2,1)S(1)} fusion(bf16[1,4096,256]{2,1,0:T(8,128)(2,1)} %param.11, bf16[1,4096,1024]{2,1,0:T(8,128)(2,1)} %all-gather.3.cloned.1.call-done), kind=kOutput, calls=%fused_computation.12 | convolution fusion | flops 2147745792 | bytes 11010048 | tf_op jit(solution)/shard_map/dot_general | solution.py:35
  82.1 2.6 gather_fusion.2
  84.7 1.4 fusion.18
  86.1 0.4 fusion.20
  86.5 1.5 pad_maximum_fusion
  88.0 2.9 %copy.13 = f32[512,1024]{1,0:T(8,128)} copy(f32[512,1024]{0,1:T(8,128)} %pad_maximum_fusion) | data formatting | bytes 4194304 | tf_op jit(solution)/shard_map/concatenate | solution.py:59
  90.9 5.3 %all-to-all-start = ((f32[16,32,1024]{2,1,0:T(8,128)}), f32[16,32,1024]{2,1,0:T(8,128)}, u32[]{:S(2)}, u32[]{:S(2)}) async-start(f32[16,32,1024]{2,1,0:T(8,128)} %bitcast.59), calls=%async_computation | async-start | bytes 4194304 | tf_op jit(solution)/shard_map/all_to_all | solution.py:14
  96.3 0.6 dynamic_slice.6
  96.9 0.6 iota_compare_fusion.4
  97.5 0.7 broadcast_compare_fusion
  98.2 25.1 %all-to-all-done = f32[16,32,1024]{2,1,0:T(8,128)} async-done(((f32[16,32,1024]{2,1,0:T(8,128)}), f32[16,32,1024]{2,1,0:T(8,128)}, u32[]{:S(2)}, u32[]{:S(2)}) %all-to-all-start) | async-done | bytes 2097184 | tf_op jit(solution)/shard_map/all_to_all | solution.py:14
  123.3 1.7 reduce_sum.18
  125.1 1.1 broadcast_in_dim.39
  126.3 8.4 %all-to-all-start.1 = ((f32[16,32,512]{2,1,0:T(8,128)}), f32[16,32,512]{2,1,0:T(8,128)S(1)}, u32[]{:S(2)}, u32[]{:S(2)}) async-start(f32[16,32,512]{2,1,0:T(8,128)} %broadcast_in_dim.39), calls=%async_computation.1 | async-start | bytes 2097152 | tf_op jit(solution)/shard_map/all_to_all | solution.py:20
  134.7 24.1 %all-to-all-done.1 = f32[16,32,512]{2,1,0:T(8,128)S(1)} async-done(((f32[16,32,512]{2,1,0:T(8,128)}), f32[16,32,512]{2,1,0:T(8,128)S(1)}, u32[]{:S(2)}, u32[]{:S(2)}) %all-to-all-start.1) | async-done | bytes 1048608 | tf_op jit(solution)/shard_map/all_to_all | solution.py:20
  158.8 0.1 multiply_reduce_fusion
  158.9 1.1 broadcast_in_dim.40
  160.1 9.9 %all-to-all-start.2 = ((f32[16,32,512]{2,1,0:T(8,128)}), f32[16,32,512]{2,1,0:T(8,128)S(1)}, u32[]{:S(2)}, u32[]{:S(2)}) async-start(f32[16,32,512]{2,1,0:T(8,128)} %broadcast_in_dim.40), calls=%async_computation.2 | async-start | bytes 2097152 | tf_op jit(solution)/shard_map/all_to_all | solution.py:20
  170.0 15.7 %all-to-all-done.2 = f32[16,32,512]{2,1,0:T(8,128)S(1)} async-done(((f32[16,32,512]{2,1,0:T(8,128)}), f32[16,32,512]{2,1,0:T(8,128)S(1)}, u32[]{:S(2)}, u32[]{:S(2)}) %all-to-all-start.2) | async-done | bytes 1048608 | tf_op jit(solution)/shard_map/all_to_all | solution.py:20
  185.6 1.3 copy.14
  187.0 1.4 fusion.16
  188.3 1.0 copy-done.1
  189.3 11.7 %cholesky.104 = f32[128,128]{1,0:T(8,128)S(1)} custom-call(f32[128,128]{1,0:T(8,128)S(1)} %cholesky.266), custom_call_target="Cholesky" | custom-call | tf_op jit(solution)/shard_map/jit(cholesky)/cholesky | solution.py:85
  201.1 0.1 cholesky.224
  201.2 9.8 %custom-call.27 = f32[1,128,128]{1,2,0:T(8,128)S(1)} custom-call(f32[1,128,128]{2,1,0:T(8,128)S(1)} %get-tuple-element.16), custom_call_target="InvertDiagBlocksLowerTriangular" | custom-call | tf_op jit(solution)/shard_map/jit(cholesky)/cholesky | solution.py:85
  211.0 1.2 constant_dynamic-update-slice_fusion.2
  212.3 1.3 convolution_subtract_fusion
  213.6 11.7 %cholesky.217 = f32[128,128]{1,0:T(8,128)S(1)} custom-call(f32[128,128]{1,0:T(8,128)S(1)} %cholesky.270), custom_call_target="Cholesky" | custom-call | tf_op jit(solution)/shard_map/jit(cholesky)/cholesky | solution.py:85
  225.3 10.0 %custom-call.28 = f32[1,128,128]{1,2,0:T(8,128)S(1)} custom-call(f32[1,128,128]{2,1,0:T(8,128)S(1)} %get-tuple-element.13), custom_call_target="InvertDiagBlocksLowerTriangular" | custom-call | tf_op jit(solution)/shard_map/jit(cholesky)/cholesky | solution.py:85
  235.3 0.3 convolution_dynamic-update-slice_fusion
  235.6 1.3 convolution_subtract_fusion.1
  236.9 11.7 %cholesky.238 = f32[128,128]{1,0:T(8,128)S(1)} custom-call(f32[128,128]{1,0:T(8,128)S(1)} %cholesky.275), custom_call_target="Cholesky" | custom-call | tf_op jit(solution)/shard_map/jit(cholesky)/cholesky | solution.py:85
  248.6 0.7 compare_reduce_fusion.1
  249.3 9.8 %custom-call.29 = f32[1,128,128]{1,2,0:T(8,128)S(1)} custom-call(f32[1,128,128]{2,1,0:T(8,128)S(1)} %get-tuple-element.10), custom_call_target="InvertDiagBlocksLowerTriangular" | custom-call | tf_op jit(solution)/shard_map/jit(cholesky)/cholesky | solution.py:85
  259.2 0.2 convolution_dynamic-update-slice_fusion.1
  259.4 1.2 convolution_subtract_fusion.2
  260.6 11.7 %cholesky.255 = f32[128,128]{1,0:T(8,128)S(1)} custom-call(f32[128,128]{1,0:T(8,128)S(1)} %convolution_subtract_fusion.2), custom_call_target="Cholesky" | custom-call | tf_op jit(solution)/shard_map/jit(cholesky)/cholesky | solution.py:85
  272.3 0.7 compare_reduce_fusion
  273.1 0.6 compare_reduce_fusion.2
  276.3 0.6 fusion.36
  (24 shorter events, 0.3 us)
Async XLA Ops:
  6.5 61.5 %copy-start = (bf16[1,4096,256]{2,1,0:T(8,128)(2,1)S(1)}, bf16[1,4096,256]{2,1,0:T(8,128)(2,1)}, u32[]{:S(2)}) copy-start(bf16[1,4096,256]{2,1,0:T(8,128)(2,1)} %param.10) | copy-start | bytes 6291460
  6.5 61.5 %all-gather.3.cloned.1.call-start = ((), (), s32[]{:S(2)}) async-start(), calls=%async_computation.3 | async-start | bytes 8912896 | tf_op jit(solution)/shard_map/all_gather | solution.py:44
  90.9 5.3 %copy-start.2 = (s32[16]{0:T(128)S(1)}, s32[16]{0:T(128)}, u32[]{:S(2)}) copy-start(s32[16]{0:T(128)} %param.14) | copy-start | bytes 196
  90.9 32.4 %all-to-all-start = ((f32[16,32,1024]{2,1,0:T(8,128)}), f32[16,32,1024]{2,1,0:T(8,128)}, u32[]{:S(2)}, u32[]{:S(2)}) async-start(f32[16,32,1024]{2,1,0:T(8,128)} %bitcast.59), calls=%async_computation | async-start | bytes 4194304 | tf_op jit(solution)/shard_map/all_to_all | solution.py:14
  125.0 9.7 %copy-start.3 = (s32[16]{0:T(128)S(1)}, s32[16]{0:T(128)}, u32[]{:S(2)}) copy-start(s32[16]{0:T(128)} %param.15) | copy-start | bytes 196
  126.3 32.5 %all-to-all-start.1 = ((f32[16,32,512]{2,1,0:T(8,128)}), f32[16,32,512]{2,1,0:T(8,128)S(1)}, u32[]{:S(2)}, u32[]{:S(2)}) async-start(f32[16,32,512]{2,1,0:T(8,128)} %broadcast_in_dim.39), calls=%async_computation.1 | async-start | bytes 2097152 | tf_op jit(solution)/shard_map/all_to_all | solution.py:20
  160.1 25.6 %all-to-all-start.2 = ((f32[16,32,512]{2,1,0:T(8,128)}), f32[16,32,512]{2,1,0:T(8,128)S(1)}, u32[]{:S(2)}, u32[]{:S(2)}) async-start(f32[16,32,512]{2,1,0:T(8,128)} %broadcast_in_dim.40), calls=%async_computation.2 | async-start | bytes 2097152 | tf_op jit(solution)/shard_map/all_to_all | solution.py:20
  188.3 1.0 copy-start.1
Sparse Core Ops, SparseCore 0:
  9.2 58.8 all-gather.2
where the time goes:
time: 284 us
  waiting for transfers between devices  120 us (42%)
  other arithmetic  85.4 us (30%)
  starting transfers between devices  23.7 us (8%)
  matrix products  19.3 us (7%)
  local copies, waits for them, and re-layouts  18.7 us (7%)
  between operations  16.3 us (6%)
    another operation x14, other arithmetic, on_device(): lower = jnp.linalg.cholesky(whole)  78.7 us
    all_gather x1, waiting for transfers between devices, on_device(): piece = lax.all_gather(vlocal, 'slab', axis=0, tiled=True)  54.8 us
    all_to_all x2, waiting for transfers between devices, from_everyone(): return lax.all_to_all(copies, axis, split_axis=0, concat_axis=0, tiled=True)  39.7 us
    all_to_all x1, waiting for transfers between devices, sum_at_owner(): lax.all_to_all(parts, axis, split_axis=0, concat_axis=0, tiled=True)  25.1 us
    all_to_all x2, starting transfers between devices, from_everyone(): return lax.all_to_all(copies, axis, split_axis=0, concat_axis=0, tiled=True)  18.4 us
    dot_general x2, matrix products, add_piece(): lax.dot_general(piece, columns, (((0,), (0,)), ((), ())), preferred_eleme...  12.1 us
  transfers between devices with their start and end apart: 4, of which 4 were waited for; matrix products, arithmetic and copies ran while one was open for 3% of the time, Pallas kernels for 0%

commit v1 on v0

--- a/solution.py
+++ b/solution.py
@@ -1,7 +1,76 @@
 import jax
 import jax.numpy as jnp
 from jax import lax
+from jax.experimental import pallas as pl
+from jax.experimental.pallas import tpu as pltpu
 from jax.sharding import PartitionSpec as P
+
+def lane_of(x, k):
+    return jnp.broadcast_to(x[:, k:k + 1], x.shape)
+
+def sub_of(x, k):
+    return jnp.broadcast_to(x[k:k + 1, :], x.shape)
+
+def panel(work, lo, p, lanes):
+    wide = [lo + 128 * v for v in range(lanes)]
+    top = lo + 8 * p
+    rows = [work[pl.ds(top, 8), pl.ds(w, 128)] for w in wide]
+    sub = lax.broadcasted_iota(jnp.int32, (8, 128), 0)
+    cols = [lane_of(rows[0], 8 * p + b) for b in range(8)]
+    scale = jnp.zeros((8, 128), jnp.float32)
+    inv, coef, urow = [], [], []
+    for k in range(8):
+        r = lax.rsqrt(sub_of(cols[k], k))
+        c = cols[k] * r
+        cs = {b: sub_of(c, b) for b in range(k + 1, 8)}
+        for b in range(k + 1, 8):
+            cols[b] = cols[b] - c * cs[b]
+        u = [sub_of(x, k) * r for x in rows]
+        cm = jnp.where(sub > k, c, 0.0)
+        rows = [x - cm * y for x, y in zip(rows, u)]
+        scale = jnp.where(sub == k, r, scale)
+        inv.append(r); coef.append(cs); urow.append(u)
+    for x, w in zip(rows, wide):
+        work[pl.ds(top, 8), pl.ds(w, 128)] = x * scale
+    for g in range(p + 1, 16):
+        at = lo + 8 * g
+        rest = [work[pl.ds(at, 8), pl.ds(w, 128)] for w in wide]
+        cols = [lane_of(rest[0], 8 * p + b) for b in range(8)]
+        for k in range(8):
+            c = cols[k] * inv[k]
+            for b in range(k + 1, 8):
+                cols[b] = cols[b] - c * coef[k][b]
+            rest = [x - c * y for x, y in zip(rest, urow[k])]
+        for x, w in zip(rest, wide):
+            work[pl.ds(at, 8), pl.ds(w, 128)] = x
+
+def factor(work, low, n):
+    blocks = n // 128
+    for j in range(blocks):
+        lo = 128 * j
+        for p in range(16):
+            panel(work, lo, p, blocks - j)
+        tri = lax.broadcasted_iota(jnp.int32, (128, 128), 0) >= lax.broadcasted_iota(jnp.int32, (128, 128), 1)
+        low[pl.ds(lo, 128), pl.ds(lo, 128)] = jnp.where(tri, work[pl.ds(lo, 128), pl.ds(lo, 128)].T, 0.0)
+        for i in range(j + 1, blocks):
+            low[pl.ds(128 * i, 128), pl.ds(lo, 128)] = work[pl.ds(lo, 128), pl.ds(128 * i, 128)].T
+            low[pl.ds(lo, 128), pl.ds(128 * i, 128)] = jnp.zeros((128, 128), jnp.float32)
+        for i in range(j + 1, blocks):
+            w = n - 128 * i
+            work[pl.ds(128 * i, 128), pl.ds(128 * i, w)] = work[pl.ds(128 * i, 128), pl.ds(128 * i, w)] - lax.dot_general(
+                low[pl.ds(128 * i, 128), pl.ds(lo, 128)], work[pl.ds(lo, 128), pl.ds(128 * i, w)],
+                (((1,), (0,)), ((), ())), preferred_element_type=jnp.float32, precision=lax.Precision.HIGHEST)
+
+def kernel(s_ref, l_ref, work):
+    n = s_ref.shape[0]
+    work[...] = s_ref[...]
+    factor(work, l_ref, n)
+
+def chol(s):
+    n = s.shape[0]
+    return pl.pallas_call(kernel, out_shape=jax.ShapeDtypeStruct((n, n), jnp.float32),
+        in_specs=[pl.BlockSpec(memory_space=pltpu.VMEM)], out_specs=pl.BlockSpec(memory_space=pltpu.VMEM),
+        scratch_shapes=[pltpu.VMEM((n, n), jnp.float32)])(s)
 
 
 def cut_along(value, dim, length):
@@ -82,7 +151,7 @@
     chosen = (dest == block_id).astype(jnp.float32)
     mine = jnp.sum(chosen[:, None, None] * everyone, axis=0)
     whole = gathered_copies(mine, "slab", 0)
-    lower = jnp.linalg.cholesky(whole)
+    lower = chol(whole)
     own = lax.dynamic_slice_in_dim(lower, row_start, share, 0)
     return own[None]
 

time: 284 us -> 215 us (0.76)
  other arithmetic: 85.4 us -> 4.76 us
  Pallas kernels: 0 us -> 19.3 us
  matrix products: 19.3 us -> 13.9 us
    another operation x14 -> x0, other arithmetic: 78.7 us -> none  [on_device(): lower = jnp.linalg.cholesky(whole)]
    pallas_call x0 -> x1, Pallas kernels: none -> 19.3 us  [chol(): pl.pallas_call(kernel, out_shape=jax.ShapeDtypeStruct((n, n), jnp.float32...]
    another operation x6 -> x0, matrix products: 5.46 us -> none  [on_device(): lower = jnp.linalg.cholesky(whole)]
  transfers between devices with their start and end apart: 4 -> 4, of which waited for: 4 -> 4; matrix products, arithmetic and copies ran while one was open for 3% -> 4% of each run, Pallas kernels for 0% -> 0%
where the time goes in v1:
time: 215 us; the launch traced here: 214 us
  waiting for transfers between devices  120 us (56%)
  starting transfers between devices  23.7 us (11%)
  Pallas kernels  19.3 us (9%)
  local copies, waits for them, and re-layouts  18.6 us (9%)
  matrix products  13.9 us (6%)
  between operations  13.6 us (6%)
  other arithmetic  4.76 us (2%)
    all_gather x1, waiting for transfers between devices, on_device(): piece = lax.all_gather(vlocal, 'slab', axis=0, tiled=True)  54.8 us
    all_to_all x2, waiting for transfers between devices, from_everyone(): return lax.all_to_all(copies, axis, split_axis=0, concat_axis=0, tiled=True)  39.7 us
    all_to_all x1, waiting for transfers between devices, sum_at_owner(): lax.all_to_all(parts, axis, split_axis=0, concat_axis=0, tiled=True)  25.1 us
    pallas_call x1, Pallas kernels, chol(): pl.pallas_call(kernel, out_shape=jax.ShapeDtypeStruct((n, n), jnp.float32...  19.3 us
    all_to_all x2, starting transfers between devices, from_everyone(): return lax.all_to_all(copies, axis, split_axis=0, concat_axis=0, tiled=True)  18.4 us
    dot_general x2, matrix products, add_piece(): lax.dot_general(piece, columns, (((0,), (0,)), ((), ())), preferred_eleme...  12.1 us
    all_to_all x1, starting transfers between devices, sum_at_owner(): lax.all_to_all(parts, axis, split_axis=0, concat_axis=0, tiled=True)  5.35 us
  transfers between devices with their start and end apart: 4, of which 4 were waited for; matrix products, arithmetic and copies ran while one was open for 4% of the time, Pallas kernels for 0%

profile of v1, /device:TPU:1, one launch (start us, length us, event | category | flops | bytes accessed | tf_op | source)
XLA Modules:
  0.0 214.2 jit_solution(1364199989095701346)
XLA Ops:
  6.5 0.0 copy-start
  6.5 0.0 all-gather.3.cloned.1.call-start
  6.5 0.7 all-gather.3.cloned.1.call-update
  7.3 1.2 copy.10
  8.5 0.8 fusion.32
  9.3 2.0 gather_fusion.1
  11.3 2.0 gather_fusion.3
  13.3 54.8 %all-gather.3.cloned.1.call-done = bf16[1,4096,1024]{2,1,0:T(8,128)(2,1)} async-done(((bf16[1,256,1024]{2,1,0:T(8,128)(2,1)}), bf16[1,4096,1024]{2,1,0:T(8,128)(2,1)}) %all-gather.3.cloned.1.call-update) | async-done | bytes 8388624 | tf_op jit(solution)/shard_map/all_gather | solution.py:113
  68.1 0.0 copy-done
  68.1 5.8 %fusion.6 = bf16[1024,256]{1,0:T(8,128)(2,1)S(1)} fusion(bf16[1,4096,256]{2,1,0:T(8,128)(2,1)S(1)} %copy-done, bf16[1,4096,1024]{2,1,0:T(8,128)(2,1)} %all-gather.3.cloned.1.call-done), kind=kOutput, calls=%fused_computation.11 | convolution fusion | flops 2147745792 | bytes 11010048 | tf_op jit(solution)/shard_map/dot_general | solution.py:104
  73.8 2.0 gather_fusion
  75.8 6.3 %fusion.11 = bf16[1024,256]{1,0:T(8,128)(2,1)S(1)} fusion(bf16[1,4096,256]{2,1,0:T(8,128)(2,1)} %param.11, bf16[1,4096,1024]{2,1,0:T(8,128)(2,1)} %all-gather.3.cloned.1.call-done), kind=kOutput, calls=%fused_computation.12 | convolution fusion | flops 2147745792 | bytes 11010048 | tf_op jit(solution)/shard_map/dot_general | solution.py:104
  82.1 2.6 %gather_fusion.2 = bf16[512,256]{1,0:T(8,128)(2,1)} fusion(bf16[1024,256]{1,0:T(8,128)(2,1)S(1)} %fusion.11, s32[1024]{0:T(1024)S(1)} %pad_clamp_fusion), kind=kCustom, calls=%fused_computation.2.clone | custom fusion | bytes 526336 | tf_op jit(solution)/shard_map/jit(_take)/gather | solution.py:126
  84.7 1.4 fusion.16
  86.1 0.4 fusion.18
  86.5 1.5 pad_maximum_fusion
  88.0 2.9 %copy.11 = f32[512,1024]{1,0:T(8,128)} copy(f32[512,1024]{0,1:T(8,128)} %pad_maximum_fusion) | data formatting | bytes 4194304 | tf_op jit(solution)/shard_map/concatenate | solution.py:128
  90.9 0.0 copy-start.2
  90.9 5.4 %all-to-all-start = ((f32[16,32,1024]{2,1,0:T(8,128)}), f32[16,32,1024]{2,1,0:T(8,128)}, u32[]{:S(2)}, u32[]{:S(2)}) async-start(f32[16,32,1024]{2,1,0:T(8,128)} %bitcast.35), calls=%async_computation | async-start | bytes 4194304 | tf_op jit(solution)/shard_map/all_to_all | solution.py:83
  96.3 0.0 copy-done.2
  96.3 0.6 dynamic_slice.6
  96.9 0.6 iota_compare_fusion.1
  97.5 0.7 broadcast_compare_fusion
  98.2 25.1 %all-to-all-done = f32[16,32,1024]{2,1,0:T(8,128)} async-done(((f32[16,32,1024]{2,1,0:T(8,128)}), f32[16,32,1024]{2,1,0:T(8,128)}, u32[]{:S(2)}, u32[]{:S(2)}) %all-to-all-start) | async-done | bytes 2097184 | tf_op jit(solution)/shard_map/all_to_all | solution.py:83
  123.3 1.7 reduce_sum.18
  125.0 0.0 copy-start.3
  125.1 0.1 fusion.29
  125.2 1.1 broadcast_in_dim.37
  126.2 8.4 %all-to-all-start.1 = ((f32[16,32,512]{2,1,0:T(8,128)}), f32[16,32,512]{2,1,0:T(8,128)S(1)}, u32[]{:S(2)}, u32[]{:S(2)}) async-start(f32[16,32,512]{2,1,0:T(8,128)} %broadcast_in_dim.37), calls=%async_computation.1 | async-start | bytes 2097152 | tf_op jit(solution)/shard_map/all_to_all | solution.py:89
  134.7 0.0 copy-done.3
  134.7 24.1 %all-to-all-done.1 = f32[16,32,512]{2,1,0:T(8,128)S(1)} async-done(((f32[16,32,512]{2,1,0:T(8,128)}), f32[16,32,512]{2,1,0:T(8,128)S(1)}, u32[]{:S(2)}, u32[]{:S(2)}) %all-to-all-start.1) | async-done | bytes 1048608 | tf_op jit(solution)/shard_map/all_to_all | solution.py:89
  158.8 0.1 multiply_reduce_fusion
  158.9 1.1 broadcast_in_dim.38
  160.0 9.9 %all-to-all-start.2 = ((f32[16,32,512]{2,1,0:T(8,128)}), f32[16,32,512]{2,1,0:T(8,128)S(1)}, u32[]{:S(2)}, u32[]{:S(2)}) async-start(f32[16,32,512]{2,1,0:T(8,128)} %broadcast_in_dim.38), calls=%async_computation.2 | async-start | bytes 2097152 | tf_op jit(solution)/shard_map/all_to_all | solution.py:89
  169.9 15.7 %all-to-all-done.2 = f32[16,32,512]{2,1,0:T(8,128)S(1)} async-done(((f32[16,32,512]{2,1,0:T(8,128)}), f32[16,32,512]{2,1,0:T(8,128)S(1)}, u32[]{:S(2)}, u32[]{:S(2)}) %all-to-all-start.2) | async-done | bytes 1048608 | tf_op jit(solution)/shard_map/all_to_all | solution.py:89
  185.6 0.0 copy-start.1
  185.6 1.0 copy-done.1
  186.6 19.3 %shard_map.64 = f32[512,512]{1,0:T(8,128)} custom-call(f32[512,512]{1,0:T(8,128)} %bitcast.36), custom_call_target="tpu_custom_call" | custom-call | tf_op jit(solution)/shard_map/pallas_call | solution.py:71
  205.9 1.5 dynamic-slice_bitcast_fusion
  (8 shorter events, 0.0 us)
Async XLA Ops:
  6.5 61.5 %copy-start = (bf16[1,4096,256]{2,1,0:T(8,128)(2,1)S(1)}, bf16[1,4096,256]{2,1,0:T(8,128)(2,1)}, u32[]{:S(2)}) copy-start(bf16[1,4096,256]{2,1,0:T(8,128)(2,1)} %param.10) | copy-start | bytes 6291460
  6.5 61.5 %all-gather.3.cloned.1.call-start = ((), (), s32[]{:S(2)}) async-start(), calls=%async_computation.3 | async-start | bytes 8912896 | tf_op jit(solution)/shard_map/all_gather | solution.py:113
  90.9 5.4 %copy-start.2 = (s32[16]{0:T(128)S(1)}, s32[16]{0:T(128)}, u32[]{:S(2)}) copy-start(s32[16]{0:T(128)} %param.14) | copy-start | bytes 196
  90.9 32.4 %all-to-all-start = ((f32[16,32,1024]{2,1,0:T(8,128)}), f32[16,32,1024]{2,1,0:T(8,128)}, u32[]{:S(2)}, u32[]{:S(2)}) async-start(f32[16,32,1024]{2,1,0:T(8,128)} %bitcast.35), calls=%async_computation | async-start | bytes 4194304 | tf_op jit(solution)/shard_map/all_to_all | solution.py:83
  125.0 9.6 %copy-start.3 = (s32[16]{0:T(128)S(1)}, s32[16]{0:T(128)}, u32[]{:S(2)}) copy-start(s32[16]{0:T(128)} %param.15) | copy-start | bytes 196
  126.2 32.5 %all-to-all-start.1 = ((f32[16,32,512]{2,1,0:T(8,128)}), f32[16,32,512]{2,1,0:T(8,128)S(1)}, u32[]{:S(2)}, u32[]{:S(2)}) async-start(f32[16,32,512]{2,1,0:T(8,128)} %broadcast_in_dim.37), calls=%async_computation.1 | async-start | bytes 2097152 | tf_op jit(solution)/shard_map/all_to_all | solution.py:89
  160.0 25.6 %all-to-all-start.2 = ((f32[16,32,512]{2,1,0:T(8,128)}), f32[16,32,512]{2,1,0:T(8,128)S(1)}, u32[]{:S(2)}, u32[]{:S(2)}) async-start(f32[16,32,512]{2,1,0:T(8,128)} %broadcast_in_dim.38), calls=%async_computation.2 | async-start | bytes 2097152 | tf_op jit(solution)/shard_map/all_to_all | solution.py:89
  185.6 1.0 copy-start.1
Sparse Core Ops, SparseCore 0:
  9.2 58.8 all-gather.2

commit v2 on v1

v2 whole, which is shorter than its diff:
```python
import jax
import jax.numpy as jnp
from jax import lax
from jax.experimental import pallas as pl
from jax.experimental.pallas import tpu as pltpu
from jax.sharding import PartitionSpec as P

MESH = pl.DeviceIdType.MESH
CHUNKS = 4
ROWS, RANK, ORDER, FOLD = 256, 1024, 512, 640
PIECE = ROWS // CHUNKS
NT = (((1,), (1,)), ((), ()))
NN = (((1,), (0,)), ((), ()))


def mm(a, b, dims):
    return lax.dot_general(a, b, dims, preferred_element_type=jnp.float32)


def folded(i):
    a = i // 8
    cut = ORDER - 128 * a
    return ((16 * i, 128 * a, 0, cut), (16 * (31 - i), 128 * (3 - a), cut, FOLD - cut))


def pair_kernel(x_hbm, y_hbm, own, index, orders, s_ref, xin, xyt, held, passing, total, pick, turned,
                part, half, mine, came, pieces, load_sem, own_sem, far_sem, near_sem, sum_sem, out_sem):
    me = lax.axis_index("slab")
    y, z, k = lax.div(me, 4), lax.rem(lax.div(me, 2), 2), lax.rem(me, 2)
    chip = 2 * y + z
    up, down, across = lax.rem(y + 1, 4), lax.rem(y + 3, 4), 1 - z

    def at(yy, zz, kk):
        return {"slab": 4 * yy + 2 * zz + kk}

    sibling, beside = at(y, z, 1 - k), at(y, across, k)
    above, below = at(up, z, k), at(down, z, k)
    others = [(dy, dz) for dy in range(4) for dz in range(2) if (dy, dz) != (0, 0)]

    def chip_at(dy, dz):
        return lax.rem(y + dy, 4), z + dz - 2 * z * dz

    def send(src, dst, sems, i, to):
        return pltpu.make_async_remote_copy(
            src_ref=src, dst_ref=dst, send_sem=sems.at[0, i], recv_sem=sems.at[1, i],
            device_id=to, device_id_type=MESH)

    w = jnp.where(y >= 2, z, across)
    groups = (chip, 2 * y + across, 2 * down + z, 2 * down + across, 2 * lax.rem(y + 2, 4) + w)
    loads = []
    for m, src in enumerate((x_hbm, y_hbm)):
        for g, c in enumerate(groups):
            copy = pltpu.make_async_copy(
                src.at[pl.ds(pl.multiple_of(512 * c, 512), 512), :], xin.at[m, g], load_sem.at[5 * m + g])
            copy.start()
            loads.append(copy)

    barrier = pltpu.get_barrier_semaphore()
    pl.semaphore_signal(barrier, inc=1, device_id=sibling, device_id_type=MESH)
    for dy, dz in others:
        yy, zz = chip_at(dy, dz)
        pl.semaphore_signal(barrier, inc=1, device_id=at(yy, zz, k), device_id_type=MESH)
    pl.semaphore_wait(barrier, 8)

    base = pl.multiple_of(ROWS * k, ROWS)

    def rows(c):
        return pl.ds(pl.multiple_of(base + PIECE * c, PIECE), PIECE)

    def bit(c):
        return pl.ds(PIECE * c, PIECE)

    own_copy = send(own, held.at[0, pl.ds(base, ROWS), :], own_sem, 0, sibling)
    own_copy.start()
    z_copy = [send(own.at[bit(c), :], held.at[1, rows(c), :], far_sem, c, beside) for c in range(CHUNKS)]
    u_copy = [send(own.at[bit(c), :], held.at[2, rows(c), :], far_sem, CHUNKS + c, above) for c in range(CHUNKS)]
    w_copy = [send(held.at[1, rows(c), :], held.at[3, rows(c), :], far_sem, 2 * CHUNKS + c, above)
              for c in range(CHUNKS)]
    p_own = [send(own.at[bit(c), :], passing.at[bit(c), :], far_sem, 3 * CHUNKS + c, below) for c in range(CHUNKS)]
    p_held = [send(held.at[1, rows(c), :], passing.at[bit(c), :], far_sem, 3 * CHUNKS + c, below)
              for c in range(CHUNKS)]
    q_copy = [send(passing.at[bit(c), :], held.at[4, rows(c), :], far_sem, 4 * CHUNKS + c, below)
              for c in range(CHUNKS)]
    near = {g: [send(held.at[g, rows(c), :], held.at[g, rows(c), :], near_sem, CHUNKS * (g - 1) + c, sibling)
                for c in range(CHUNKS)] for g in (1, 2, 3, 4)}
    for c in range(CHUNKS):
        z_copy[c].start()
        u_copy[c].start()

    @pl.when(y < 2)
    def _():
        for c in range(CHUNKS):
            p_own[c].start()

    held[0, pl.ds(base, ROWS), :] = own[...]
    for m in range(2):
        wanted = jnp.broadcast_to(index[m:m + 1, :], (128, ORDER)).astype(jnp.float32).T
        for j in range(RANK // 128):
            lane = lax.broadcasted_iota(jnp.int32, (ORDER, 128), 1).astype(jnp.float32) + 128.0 * j
            pick[m, :, 128 * j:128 * j + 128] = jnp.where(wanted == lane, 1.0, 0.0).astype(jnp.bfloat16)
        turned[m, :, 256:512] = mm(pick[m], own[...], NT).astype(jnp.bfloat16)
    for copy in loads:
        copy.wait()
    for m in range(2):
        for g in range(5):
            xt = xin[m, g].T
            if g < 2:
                xt = xt * jnp.bfloat16(0.5)
            xyt[256 * m:256 * m + 256, 512 * g:512 * g + 512] = xt

    def gather_step(g, first=False):
        for j in range(RANK // 256):
            cols = slice(256 * j, 256 * j + 256)
            more = mm(xyt[:, 512 * g:512 * g + 512], held[g, :, cols], NN)
            total[:, cols] = more if first else total[:, cols] + more

    own_copy.wait_recv()
    gather_step(0, first=True)
    for c in range(CHUNKS):
        z_copy[c].wait_recv()
        w_copy[c].start()
        near[1][c].start()

        @pl.when(y >= 2)
        def _():
            p_held[c].start()

        p_own[c].wait_recv()
        q_copy[c].start()
    for c in range(CHUNKS):
        u_copy[c].wait_recv()
        near[2][c].start()
    for g in (1, 2):
        for c in range(CHUNKS):
            near[g][c].wait_recv()
        gather_step(g)
    for c in range(CHUNKS):
        w_copy[c].wait_recv()
        near[3][c].start()
        q_copy[c].wait_recv()
        near[4][c].start()
    for g in (3, 4):
        for c in range(CHUNKS):
            near[g][c].wait_recv()
        gather_step(g)

    half_copy = []
    for m in range(2):
        cxt = total[256 * m:256 * m + 256, :].astype(jnp.bfloat16)
        turned[m, :, 0:256] = mm(pick[m], cxt, NT).astype(jnp.bfloat16)
        for j in range(4):
            lo = 128 * j
            block = (mm(turned[m, lo:lo + 128, 0:256], turned[m, lo:, 256:512], NT)
                     + mm(turned[m, lo:lo + 128, 256:512], turned[m, lo:, 0:256], NT))
            for i in range(16):
                for row, col, lane, width in folded(i):
                    if lo <= row < lo + 128:
                        part[m, i % 2, i // 2, :, lane:lane + width] = block[row - lo:row - lo + 16, col - lo:]
        copy = send(part.at[m, 1 - k], half.at[m], sum_sem, m, sibling)
        copy.start()
        half_copy.append(copy)
    for m in range(2):
        half_copy[m].wait_recv()
        mine[:, :, FOLD * m:FOLD * m + FOLD] = part[m, k] + half[m]
    sums = []
    for n, (dy, dz) in enumerate(others):
        yy, zz = chip_at(dy, dz)
        copy = send(mine.at[2 * yy + zz], came.at[n], sum_sem, 2 + n, at(yy, zz, k))
        copy.start()
        sums.append(copy)
    both = mine[chip]
    for n in range(7):
        sums[n].wait_recv()
        both = both + came[n]

    lane = lax.broadcasted_iota(jnp.int32, (16, FOLD), 1)
    line = lax.broadcasted_iota(jnp.int32, (16, FOLD), 0)
    a = lax.div(me, 8)
    cut = ORDER - 128 * a
    low_part = lane < cut
    row = jnp.where(low_part, 16 * me, 16 * (31 - me)) + line
    col = jnp.where(low_part, 128 * a + lane, 128 * (3 - a) + lane - cut)
    order = orders[lax.axis_index("blk")]
    live = (row < order) & (col < order)
    pieces[me] = jnp.where(live, both[:, :FOLD] * both[:, FOLD:], 0.0) + jnp.where(row == col, 1.0, 0.0)

    outs = [send(pieces.at[me], pieces.at[me], out_sem, 0, sibling)]
    for n, (dy, dz) in enumerate(others):
        yy, zz = chip_at(dy, dz)
        outs.append(send(pieces.at[me], pieces.at[me], out_sem, 1 + n, at(yy, zz, k)))
    for copy in outs:
        copy.start()
    passed = []
    for n, (dy, dz) in enumerate(others):
        yy, zz = chip_at(4 - dy, dz)
        source = 4 * yy + 2 * zz + k
        outs[1 + n].wait_recv()
        copy = send(pieces.at[source], pieces.at[source], out_sem, 8 + n, sibling)
        copy.start()
        passed.append(copy)
    outs[0].wait_recv()
    for copy in passed:
        copy.wait_recv()
    for i in range(16):
        for row, col, lane, width in folded(i):
            s_ref[row:row + 16, col:col + width] = pieces[i, :, lane:lane + width]

    own_copy.wait_send()
    for copies in (z_copy, u_copy, w_copy, p_own, q_copy, near[1], near[2], near[3], near[4], half_copy, sums,
                   outs, passed):
        for copy in copies:
            copy.wait_send()


def schur_rows(x, y, v, index, orders):
    bf, f32 = jnp.bfloat16, jnp.float32
    vm, dma = pltpu.VMEM, pltpu.SemaphoreType.DMA
    return pl.pallas_call(
        pair_kernel,
        out_shape=jax.ShapeDtypeStruct((ORDER, ORDER), f32),
        in_specs=[pl.BlockSpec(memory_space=pl.ANY)] * 2 + [pl.BlockSpec(memory_space=vm)] * 2
        + [pl.BlockSpec(memory_space=pltpu.SMEM)],
        out_specs=pl.BlockSpec(memory_space=vm),
        scratch_shapes=[
            vm((2, 5, 512, 256), bf), vm((512, 2560), bf), vm((5, 512, RANK), bf), vm((ROWS, RANK), bf),
            vm((512, RANK), f32), vm((2, ORDER, RANK), bf), vm((2, ORDER, 512), bf),
            vm((2, 2, 8, 16, FOLD), f32), vm((2, 8, 16, FOLD), f32), vm((8, 16, 2 * FOLD), f32),
            vm((7, 16, 2 * FOLD), f32), vm((16, 16, FOLD), f32),
            dma((10,)), dma((2, 1)), dma((2, 5 * CHUNKS)), dma((2, 4 * CHUNKS)), dma((2, 9)), dma((2, 15)),
        ],
        compiler_params=pltpu.CompilerParams(collective_id=0, has_side_effects=True),
    )(x, y, v, index, orders)


def lane_of(x, k):
    return jnp.broadcast_to(x[:, k:k + 1], x.shape)


def sub_of(x, k):
    return jnp.broadcast_to(x[k:k + 1, :], x.shape)


def panel(work, lo, p, lanes):
    wide = [lo + 128 * v for v in range(lanes)]
    top = lo + 8 * p
    rows = [work[pl.ds(top, 8), pl.ds(w, 128)] for w in wide]
    sub = lax.broadcasted_iota(jnp.int32, (8, 128), 0)
    cols = [lane_of(rows[0], 8 * p + b) for b in range(8)]
    scale = jnp.zeros((8, 128), jnp.float32)
    inv, coef, urow = [], [], []
    for k in range(8):
        r = lax.rsqrt(sub_of(cols[k], k))
        c = cols[k] * r
        cs = {b: sub_of(c, b) for b in range(k + 1, 8)}
        for b in range(k + 1, 8):
            cols[b] = cols[b] - c * cs[b]
        u = [sub_of(x, k) * r for x in rows]
        cm = jnp.where(sub > k, c, 0.0)
        rows = [x - cm * y for x, y in zip(rows, u)]
        scale = jnp.where(sub == k, r, scale)
        inv.append(r); coef.append(cs); urow.append(u)
    for x, w in zip(rows, wide):
        work[pl.ds(top, 8), pl.ds(w, 128)] = x * scale
    for g in range(p + 1, 16):
        at = lo + 8 * g
        rest = [work[pl.ds(at, 8), pl.ds(w, 128)] for w in wide]
        cols = [lane_of(rest[0], 8 * p + b) for b in range(8)]
        for k in range(8):
            c = cols[k] * inv[k]
            for b in range(k + 1, 8):
                cols[b] = cols[b] - c * coef[k][b]
            rest = [x - c * y for x, y in zip(rest, urow[k])]
        for x, w in zip(rest, wide):
            work[pl.ds(at, 8), pl.ds(w, 128)] = x


def factor(work, low, n):
    blocks = n // 128
    for j in range(blocks):
        lo = 128 * j
        for p in range(16):
            panel(work, lo, p, blocks - j)
        tri = lax.broadcasted_iota(jnp.int32, (128, 128), 0) >= lax.broadcasted_iota(jnp.int32, (128, 128), 1)
        low[pl.ds(lo, 128), pl.ds(lo, 128)] = jnp.where(tri, work[pl.ds(lo, 128), pl.ds(lo, 128)].T, 0.0)
        for i in range(j + 1, blocks):
            low[pl.ds(128 * i, 128), pl.ds(lo, 128)] = work[pl.ds(lo, 128), pl.ds(128 * i, 128)].T
            low[pl.ds(lo, 128), pl.ds(128 * i, 128)] = jnp.zeros((128, 128), jnp.float32)
        for i in range(j + 1, blocks):
            w = n - 128 * i
            work[pl.ds(128 * i, 128), pl.ds(128 * i, w)] = work[pl.ds(128 * i, 128), pl.ds(128 * i, w)] - lax.dot_general(
                low[pl.ds(128 * i, 128), pl.ds(lo, 128)], work[pl.ds(lo, 128), pl.ds(128 * i, w)],
                (((1,), (0,)), ((), ())), preferred_element_type=jnp.float32, precision=lax.Precision.HIGHEST)


def chol_kernel(s_ref, own_ref, work, low):
    n, share = s_ref.shape[0], own_ref.shape[0]
    work[...] = s_ref[...]
    factor(work, low, n)
    own_ref[...] = low[pl.ds(pl.multiple_of(share * lax.axis_index("slab"), share), share), :]


def chol_rows(s, share):
    n = s.shape[0]
    return pl.pallas_call(
        chol_kernel,
        out_shape=jax.ShapeDtypeStruct((share, n), jnp.float32),
        in_specs=[pl.BlockSpec(memory_space=pltpu.VMEM)],
        out_specs=pl.BlockSpec(memory_space=pltpu.VMEM),
        scratch_shapes=[pltpu.VMEM((n, n), jnp.float32)] * 2,
    )(s)


def route_kernel(l_ref, dest, out_ref, along, sent, came, x_sem, z_sem):
    me = lax.axis_index("blk")
    x, h = lax.div(me, 4), lax.rem(me, 4)

    def send(src, dst, sems, i, to):
        return pltpu.make_async_remote_copy(
            src_ref=src, dst_ref=dst, send_sem=sems.at[0, i], recv_sem=sems.at[1, i],
            device_id={"blk": to}, device_id_type=MESH)

    def x_at(d):
        return 4 * lax.rem(x + d, 4) + h

    def h_at(d):
        return 4 * x + lax.rem(h + d, 4)

    barrier = pltpu.get_barrier_semaphore()
    for d in (1, 2, 3):
        for to in (x_at(d), h_at(d)):
            pl.semaphore_signal(barrier, inc=1, device_id={"blk": to}, device_id_type=MESH)
    pl.semaphore_wait(barrier, 6)
    first = [send(l_ref, along.at[d - 1], x_sem, d - 1, x_at(d)) for d in (1, 2, 3)]
    for copy in first:
        copy.start()
    have = [(me, l_ref[...])]
    for d in (1, 2, 3):
        first[d - 1].wait_recv()
        have.append((x_at(4 - d), along[d - 1]))

    def bound_for(to):
        kept = jnp.zeros(l_ref.shape, jnp.float32)
        for block, value in have:
            kept = jnp.where(dest[block] == to, value, kept)
        return kept

    second = []
    for d in (2, 1, 3):
        sent[d - 1] = bound_for(h_at(d))
        copy = send(sent.at[d - 1], came.at[d - 1], z_sem, d - 1, h_at(d))
        copy.start()
        second.append((d, copy))
    result = bound_for(me)
    for d, copy in second:
        copy.wait_recv()
        result = result + came[d - 1]
    out_ref[0] = result
    for copy in first + [c for _, c in second]:
        copy.wait_send()


def route(rows, dest):
    vm, dma = pltpu.VMEM, pltpu.SemaphoreType.DMA
    return pl.pallas_call(
        route_kernel,
        out_shape=jax.ShapeDtypeStruct((1, *rows.shape), jnp.float32),
        in_specs=[pl.BlockSpec(memory_space=vm), pl.BlockSpec(memory_space=pltpu.SMEM)],
        out_specs=pl.BlockSpec(memory_space=vm),
        scratch_shapes=[vm((3, *rows.shape), jnp.float32)] * 3 + [dma((2, 3)), dma((2, 3))],
        compiler_params=pltpu.CompilerParams(collective_id=1, has_side_effects=True),
    )(rows, dest)


def on_device(xinv, ymat, basis, pair_index, orders, dest):
    whole = schur_rows(xinv[0], ymat[0], basis[0], pair_index[0], orders)
    rows = chol_rows(whole, ORDER // lax.axis_size("slab"))
    return route(rows, dest)


def solution(mesh):
    return jax.shard_map(
        on_device,
        mesh=mesh,
        in_specs=(
            P("blk", None, "slab"),
            P("blk", None, "slab"),
            P("blk", "slab", None),
            P("blk", None, None),
            P(),
            P(),
        ),
        out_specs=P("blk", "slab", None),
        check_vma=False,
    )
```

time: 215 us -> 104 us (0.48)
  waiting for transfers between devices: 120 us -> 0 us
  Pallas kernels: 19.3 us -> 102 us
  starting transfers between devices: 23.7 us -> 0 us
  local copies, waits for them, and re-layouts: 18.6 us -> 1.47 us
  matrix products: 13.9 us -> 0 us
  between operations: 13.6 us -> 0.02 us
  other arithmetic: 4.76 us -> 0 us
    pallas_call x1 -> x3, Pallas kernels: 19.3 us -> 102 us  [the longest x1 62.7 us: schur_rows(): pl.pallas_call(pair_kernel, out_shape=jax.ShapeDtypeStruct((ORDER, ORDER)...]
    all_to_all x3 -> x0, waiting for transfers between devices: 64.9 us -> none  [the longest x2 39.7 us: from_everyone(): return lax.all_to_all(copies, axis, split_axis=0, concat_axis=0, tiled=True)]
    all_gather x1 -> x0, waiting for transfers between devices: 54.8 us -> none  [on_device(): piece = lax.all_gather(vlocal, 'slab', axis=0, tiled=True)]
    all_to_all x3 -> x0, starting transfers between devices: 23.7 us -> none  [the longest x2 18.4 us: from_everyone(): return lax.all_to_all(copies, axis, split_axis=0, concat_axis=0, tiled=True)]
    dot_general x4 -> x0, matrix products: 13.9 us -> none  [the longest x2 12.1 us: add_piece(): lax.dot_general(piece, columns, (((0,), (0,)), ((), ())), preferred_eleme...]
    gather x4 -> x0, local copies, waits for them, and re-layouts: 8.44 us -> none  [the longest x1 2.58 us: on_device(): cy_second = jnp.take(cy, second, axis=0)]
    broadcast_in_dim x3 -> x0, local copies, waits for them, and re-layouts: 3.66 us -> none  [the longest x2 2.19 us: from_everyone(): copies = jnp.broadcast_to(value, (lax.axis_size(axis), *value.shape))]
    concatenate x1 -> x0, local copies, waits for them, and re-layouts: 2.94 us -> none  [on_device(): jnp.concatenate([jnp.dot(cx_first, basis_first, preferred_element_type=jn...]
  transfers between devices with their start and end apart: 4 -> 0, of which waited for: 4 -> 0; matrix products, arithmetic and copies ran while one was open for 4% -> 0% of each run, Pallas kernels for 0% -> 0%
where the time goes in v2:
time: 104 us; the launch traced here: 103 us
  Pallas kernels  102 us (98%)
  local copies, waits for them, and re-layouts  1.47 us (1%)
    pallas_call x1, Pallas kernels, schur_rows(): pl.pallas_call(pair_kernel, out_shape=jax.ShapeDtypeStruct((ORDER, ORDER)...  62.7 us
    pallas_call x1, Pallas kernels, route(): pl.pallas_call(route_kernel, out_shape=jax.ShapeDtypeStruct((1, *rows.sha...  20.1 us
    pallas_call x1, Pallas kernels, chol_rows(): pl.pallas_call(chol_kernel, out_shape=jax.ShapeDtypeStruct((share, n), jn...  19.1 us

profile of v2, /device:TPU:1, one launch (start us, length us, event | category | flops | bytes accessed | tf_op | source)
XLA Modules:
  0.0 103.4 jit_solution(1414245407223726975)
XLA Ops:
  0.0 62.7 %shard_map.64.s_ref = f32[512,512]{1,0:T(8,128)} custom-call(bf16[4096,256]{1,0:T(8,128)(2,1)} %bitcast.4, bf16[4096,256]{1,0:T(8,128)(2,1)} %bitcast.5, bf16[256,1024]{1,0:T(8,128)(2,1)} %bitcast.6, s32[2,512]{1,0:T(2,128)} %bitcast.7, s32[16]{0:T(128)} %orders.1), custom_call_target="tpu_custom_call" | custom-call | tf_op jit(solution)/shard_map/pallas_call | solution.py:218
  62.7 19.1 %shard_map.65.l_ref = f32[32,512]{1,0:T(8,128)} custom-call(f32[512,512]{1,0:T(8,128)} %shard_map.64.s_ref), custom_call_target="tpu_custom_call" | custom-call | tf_op jit(solution)/shard_map/pallas_call | solution.py:304
  81.8 20.1 %shard_map.66 = f32[1,32,512]{2,1,0:T(8,128)} custom-call(f32[32,512]{1,0:T(8,128)} %shard_map.65.l_ref, s32[16]{0:T(128)} %dest.1), custom_call_target="tpu_custom_call" | custom-call | tf_op jit(solution)/shard_map/pallas_call | solution.py:364
  101.9 1.5 %copy.8 = f32[1,32,512]{2,1,0:T(8,128)} copy(f32[1,32,512]{2,1,0:T(8,128)} %shard_map.66) | data formatting | bytes 131072

commit v3 on v2

--- a/solution.py
+++ b/solution.py
@@ -23,18 +23,22 @@
     return ((16 * i, 128 * a, 0, cut), (16 * (31 - i), 128 * (3 - a), cut, FOLD - cut))
 
 
-def pair_kernel(x_hbm, y_hbm, own, index, orders, s_ref, xin, xyt, held, passing, total, pick, turned,
-                part, half, mine, came, pieces, load_sem, own_sem, far_sem, near_sem, sum_sem, out_sem):
+def pair_kernel(x_hbm, y_hbm, own, index, orders, dest, s_ref, xin, xyt, held, total, pick, turned,
+                part, half, mine, came, formed, along, bound, brought, pieces,
+                load_sem, own_sem, far_sem, near_sem, sum_sem, x_sem, h_sem, out_sem):
     me = lax.axis_index("slab")
     y, z, k = lax.div(me, 4), lax.rem(lax.div(me, 2), 2), lax.rem(me, 2)
     chip = 2 * y + z
+    group = lax.axis_index("blk")
+    bx, bh = lax.div(group, 4), lax.rem(group, 4)
     up, down, across = lax.rem(y + 1, 4), lax.rem(y + 3, 4), 1 - z
 
     def at(yy, zz, kk):
         return {"slab": 4 * yy + 2 * zz + kk}
 
     sibling, beside = at(y, z, 1 - k), at(y, across, k)
-    above, below = at(up, z, k), at(down, z, k)
+    above, below, slant = at(up, z, k), at(down, z, k), at(down, across, k)
+    opposite = at(lax.rem(y + 2, 4), z, k)
     others = [(dy, dz) for dy in range(4) for dz in range(2) if (dy, dz) != (0, 0)]
 
     def chip_at(dy, dz):
@@ -45,8 +49,14 @@
             src_ref=src, dst_ref=dst, send_sem=sems.at[0, i], recv_sem=sems.at[1, i],
             device_id=to, device_id_type=MESH)
 
+    def x_at(d):
+        return 4 * lax.rem(bx + d, 4) + bh
+
+    def h_at(d):
+        return 4 * bx + lax.rem(bh + d, 4)
+
     w = jnp.where(y >= 2, z, across)
-    groups = (chip, 2 * y + across, 2 * down + z, 2 * down + across, 2 * lax.rem(y + 2, 4) + w)
+    groups = (chip, 2 * y + across, 2 * down + z, 2 * up + across, 2 * lax.rem(y + 2, 4) + w)
     loads = []
     for m, src in enumerate((x_hbm, y_hbm)):
         for g, c in enumerate(groups):
@@ -60,7 +70,10 @@
     for dy, dz in others:
         yy, zz = chip_at(dy, dz)
         pl.semaphore_signal(barrier, inc=1, device_id=at(yy, zz, k), device_id_type=MESH)
-    pl.semaphore_wait(barrier, 8)
+    for d in (1, 2, 3):
+        for to in (x_at(d), h_at(d)):
+            pl.semaphore_signal(barrier, inc=1, device_id={"blk": to}, device_id_type=MESH)
+    pl.semaphore_wait(barrier, 14)
 
     base = pl.multiple_of(ROWS * k, ROWS)
 
@@ -74,18 +87,19 @@
     own_copy.start()
     z_copy = [send(own.at[bit(c), :], held.at[1, rows(c), :], far_sem, c, beside) for c in range(CHUNKS)]
     u_copy = [send(own.at[bit(c), :], held.at[2, rows(c), :], far_sem, CHUNKS + c, above) for c in range(CHUNKS)]
-    w_copy = [send(held.at[1, rows(c), :], held.at[3, rows(c), :], far_sem, 2 * CHUNKS + c, above)
-              for c in range(CHUNKS)]
-    p_own = [send(own.at[bit(c), :], passing.at[bit(c), :], far_sem, 3 * CHUNKS + c, below) for c in range(CHUNKS)]
-    p_held = [send(held.at[1, rows(c), :], passing.at[bit(c), :], far_sem, 3 * CHUNKS + c, below)
-              for c in range(CHUNKS)]
-    q_copy = [send(passing.at[bit(c), :], held.at[4, rows(c), :], far_sem, 4 * CHUNKS + c, below)
+    w_copy = [send(held.at[1, rows(c), :] if c < CHUNKS // 2 else own.at[bit(c), :], held.at[3, rows(c), :],
+                   far_sem, 2 * CHUNKS + c, below if c < CHUNKS // 2 else slant) for c in range(CHUNKS)]
+    p_own = [send(own.at[bit(c), :], held.at[4, rows(c), :], far_sem, 3 * CHUNKS + c, opposite)
+             for c in range(CHUNKS)]
+    p_held = [send(held.at[1, rows(c), :], held.at[4, rows(c), :], far_sem, 3 * CHUNKS + c, opposite)
               for c in range(CHUNKS)]
     near = {g: [send(held.at[g, rows(c), :], held.at[g, rows(c), :], near_sem, CHUNKS * (g - 1) + c, sibling)
                 for c in range(CHUNKS)] for g in (1, 2, 3, 4)}
     for c in range(CHUNKS):
         z_copy[c].start()
         u_copy[c].start()
+    for c in range(CHUNKS // 2, CHUNKS):
+        w_copy[c].start()
 
     @pl.when(y < 2)
     def _():
@@ -118,26 +132,27 @@
     gather_step(0, first=True)
     for c in range(CHUNKS):
         z_copy[c].wait_recv()
-        w_copy[c].start()
-        near[1][c].start()
+        if c < CHUNKS // 2:
+            w_copy[c].start()
 
         @pl.when(y >= 2)
         def _():
             p_held[c].start()
 
-        p_own[c].wait_recv()
-        q_copy[c].start()
+        near[1][c].start()
+    for c in range(CHUNKS):
+        near[1][c].wait_recv()
+    gather_step(1)
     for c in range(CHUNKS):
         u_copy[c].wait_recv()
         near[2][c].start()
-    for g in (1, 2):
-        for c in range(CHUNKS):
-            near[g][c].wait_recv()
-        gather_step(g)
+    for c in range(CHUNKS):
+        near[2][c].wait_recv()
+    gather_step(2)
     for c in range(CHUNKS):
         w_copy[c].wait_recv()
         near[3][c].start()
-        q_copy[c].wait_recv()
+        p_own[c].wait_recv()
         near[4][c].start()
     for g in (3, 4):
         for c in range(CHUNKS):
@@ -159,19 +174,22 @@
         copy = send(part.at[m, 1 - k], half.at[m], sum_sem, m, sibling)
         copy.start()
         half_copy.append(copy)
+    sums = [[], []]
     for m in range(2):
         half_copy[m].wait_recv()
-        mine[:, :, FOLD * m:FOLD * m + FOLD] = part[m, k] + half[m]
-    sums = []
-    for n, (dy, dz) in enumerate(others):
-        yy, zz = chip_at(dy, dz)
-        copy = send(mine.at[2 * yy + zz], came.at[n], sum_sem, 2 + n, at(yy, zz, k))
-        copy.start()
-        sums.append(copy)
-    both = mine[chip]
-    for n in range(7):
-        sums[n].wait_recv()
-        both = both + came[n]
+        mine[m] = part[m, k] + half[m]
+        for n, (dy, dz) in enumerate(others):
+            yy, zz = chip_at(dy, dz)
+            copy = send(mine.at[m, 2 * yy + zz], came.at[m, n], sum_sem, 2 + 7 * m + n, at(yy, zz, k))
+            copy.start()
+            sums[m].append(copy)
+    both = []
+    for m in range(2):
+        whole = mine[m, chip]
+        for n in range(7):
+            sums[m][n].wait_recv()
+            whole = whole + came[m, n]
+        both.append(whole)
 
     lane = lax.broadcasted_iota(jnp.int32, (16, FOLD), 1)
     line = lax.broadcasted_iota(jnp.int32, (16, FOLD), 0)
@@ -180,9 +198,35 @@
     low_part = lane < cut
     row = jnp.where(low_part, 16 * me, 16 * (31 - me)) + line
     col = jnp.where(low_part, 128 * a + lane, 128 * (3 - a) + lane - cut)
-    order = orders[lax.axis_index("blk")]
+    order = orders[group]
     live = (row < order) & (col < order)
-    pieces[me] = jnp.where(live, both[:, :FOLD] * both[:, FOLD:], 0.0) + jnp.where(row == col, 1.0, 0.0)
+    formed[...] = jnp.where(live, both[0] * both[1], 0.0) + jnp.where(row == col, 1.0, 0.0)
+
+    first = [send(formed, along.at[d - 1], x_sem, d - 1, {"blk": x_at(d)}) for d in (1, 2, 3)]
+    for copy in first:
+        copy.start()
+    have = [(group, formed[...])]
+    for d in (1, 2, 3):
+        first[d - 1].wait_recv()
+        have.append((x_at(4 - d), along[d - 1]))
+
+    def bound_for(to):
+        kept = jnp.zeros((16, FOLD), jnp.float32)
+        for source, value in have:
+            kept = jnp.where(dest[source] == to, value, kept)
+        return kept
+
+    second = []
+    for d in (2, 1, 3):
+        bound[d - 1] = bound_for(h_at(d))
+        copy = send(bound.at[d - 1], brought.at[d - 1], h_sem, d - 1, {"blk": h_at(d)})
+        copy.start()
+        second.append((d, copy))
+    here = bound_for(group)
+    for d, copy in second:
+        copy.wait_recv()
+        here = here + brought[d - 1]
+    pieces[me] = here
 
     outs = [send(pieces.at[me], pieces.at[me], out_sem, 0, sibling)]
     for n, (dy, dz) in enumerate(others):
@@ -206,30 +250,32 @@
             s_ref[row:row + 16, col:col + width] = pieces[i, :, lane:lane + width]
 
     own_copy.wait_send()
-    for copies in (z_copy, u_copy, w_copy, p_own, q_copy, near[1], near[2], near[3], near[4], half_copy, sums,
-                   outs, passed):
+    for copies in (z_copy, u_copy, w_copy, p_own, near[1], near[2], near[3], near[4], half_copy, *sums, first,
+                   [copy for _, copy in second], outs, passed):
         for copy in copies:
             copy.wait_send()
 
 
-def schur_rows(x, y, v, index, orders):
+def schur_block(x, y, v, index, orders, dest):
     bf, f32 = jnp.bfloat16, jnp.float32
     vm, dma = pltpu.VMEM, pltpu.SemaphoreType.DMA
     return pl.pallas_call(
         pair_kernel,
         out_shape=jax.ShapeDtypeStruct((ORDER, ORDER), f32),
         in_specs=[pl.BlockSpec(memory_space=pl.ANY)] * 2 + [pl.BlockSpec(memory_space=vm)] * 2
-        + [pl.BlockSpec(memory_space=pltpu.SMEM)],
+        + [pl.BlockSpec(memory_space=pltpu.SMEM)] * 2,
         out_specs=pl.BlockSpec(memory_space=vm),
         scratch_shapes=[
-            vm((2, 5, 512, 256), bf), vm((512, 2560), bf), vm((5, 512, RANK), bf), vm((ROWS, RANK), bf),
+            vm((2, 5, 512, 256), bf), vm((512, 2560), bf), vm((5, 512, RANK), bf),
             vm((512, RANK), f32), vm((2, ORDER, RANK), bf), vm((2, ORDER, 512), bf),
-            vm((2, 2, 8, 16, FOLD), f32), vm((2, 8, 16, FOLD), f32), vm((8, 16, 2 * FOLD), f32),
-            vm((7, 16, 2 * FOLD), f32), vm((16, 16, FOLD), f32),
-            dma((10,)), dma((2, 1)), dma((2, 5 * CHUNKS)), dma((2, 4 * CHUNKS)), dma((2, 9)), dma((2, 15)),
+            vm((2, 2, 8, 16, FOLD), f32), vm((2, 8, 16, FOLD), f32), vm((2, 8, 16, FOLD), f32),
+            vm((2, 7, 16, FOLD), f32), vm((16, FOLD), f32), vm((3, 16, FOLD), f32), vm((3, 16, FOLD), f32),
+            vm((3, 16, FOLD), f32), vm((16, 16, FOLD), f32),
+            dma((10,)), dma((2, 1)), dma((2, 4 * CHUNKS)), dma((2, 4 * CHUNKS)), dma((2, 16)),
+            dma((2, 3)), dma((2, 3)), dma((2, 15)),
         ],
         compiler_params=pltpu.CompilerParams(collective_id=0, has_side_effects=True),
-    )(x, y, v, index, orders)
+    )(x, y, v, index, orders, dest)
 
 
 def lane_of(x, k):
@@ -310,71 +356,9 @@
     )(s)
 
 
-def route_kernel(l_ref, dest, out_ref, along, sent, came, x_sem, z_sem):
-    me = lax.axis_index("blk")
-    x, h = lax.div(me, 4), lax.rem(me, 4)
-
-    def send(src, dst, sems, i, to):
-        return pltpu.make_async_remote_copy(
-            src_ref=src, dst_ref=dst, send_sem=sems.at[0, i], recv_sem=sems.at[1, i],
-            device_id={"blk": to}, device_id_type=MESH)
-
-    def x_at(d):
-        return 4 * lax.rem(x + d, 4) + h
-
-    def h_at(d):
-        return 4 * x + lax.rem(h + d, 4)
-
-    barrier = pltpu.get_barrier_semaphore()
-    for d in (1, 2, 3):
-        for to in (x_at(d), h_at(d)):
-            pl.semaphore_signal(barrier, inc=1, device_id={"blk": to}, device_id_type=MESH)
-    pl.semaphore_wait(barrier, 6)
-    first = [send(l_ref, along.at[d - 1], x_sem, d - 1, x_at(d)) for d in (1, 2, 3)]
-    for copy in first:
-        copy.start()
-    have = [(me, l_ref[...])]
-    for d in (1, 2, 3):
-        first[d - 1].wait_recv()
-        have.append((x_at(4 - d), along[d - 1]))
-
-    def bound_for(to):
-        kept = jnp.zeros(l_ref.shape, jnp.float32)
-        for block, value in have:
-            kept = jnp.where(dest[block] == to, value, kept)
-        return kept
-
-    second = []
-    for d in (2, 1, 3):
-        sent[d - 1] = bound_for(h_at(d))
-        copy = send(sent.at[d - 1], came.at[d - 1], z_sem, d - 1, h_at(d))
-        copy.start()
-        second.append((d, copy))
-    result = bound_for(me)
-    for d, copy in second:
-        copy.wait_recv()
-        result = result + came[d - 1]
-    out_ref[0] = result
-    for copy in first + [c for _, c in second]:
-        copy.wait_send()
-
-
-def route(rows, dest):
-    vm, dma = pltpu.VMEM, pltpu.SemaphoreType.DMA
-    return pl.pallas_call(
-        route_kernel,
-        out_shape=jax.ShapeDtypeStruct((1, *rows.shape), jnp.float32),
-        in_specs=[pl.BlockSpec(memory_space=vm), pl.BlockSpec(memory_space=pltpu.SMEM)],
-        out_specs=pl.BlockSpec(memory_space=vm),
-        scratch_shapes=[vm((3, *rows.shape), jnp.float32)] * 3 + [dma((2, 3)), dma((2, 3))],
-        compiler_params=pltpu.CompilerParams(collective_id=1, has_side_effects=True),
-    )(rows, dest)
-
-
 def on_device(xinv, ymat, basis, pair_index, orders, dest):
-    whole = schur_rows(xinv[0], ymat[0], basis[0], pair_index[0], orders)
-    rows = chol_rows(whole, ORDER // lax.axis_size("slab"))
-    return route(rows, dest)
+    whole = schur_block(xinv[0], ymat[0], basis[0], pair_index[0], orders, dest)
+    return chol_rows(whole, ORDER // lax.axis_size("slab"))[None]
 
 
 def solution(mesh):

time: 104 us -> 91.7 us (0.88)
  Pallas kernels: 102 us -> 91.5 us
  local copies, waits for them, and re-layouts: 1.47 us -> 0 us
    pallas_call x2 -> x1, Pallas kernels: 82.8 us -> 72.4 us  [schur_block(): pl.pallas_call(pair_kernel, out_shape=jax.ShapeDtypeStruct((ORDER, ORDER)...]
    unnamed x1 -> x0, local copies, waits for them, and re-layouts: 1.47 us -> none
where the time goes in v3:
time: 91.7 us; the launch traced here: 91.5 us
  Pallas kernels  91.5 us (100%)
    pallas_call x1, Pallas kernels, schur_block(): pl.pallas_call(pair_kernel, out_shape=jax.ShapeDtypeStruct((ORDER, ORDER)...  72.4 us
    pallas_call x1, Pallas kernels, chol_rows(): pl.pallas_call(chol_kernel, out_shape=jax.ShapeDtypeStruct((share, n), jn...  19.1 us

profile of v3, /device:TPU:1, one launch (start us, length us, event | category | flops | bytes accessed | tf_op | source)
XLA Modules:
  0.0 91.5 jit_solution(13369630123407905940)
XLA Ops:
  0.0 72.4 %shard_map.64.s_ref = f32[512,512]{1,0:T(8,128)} custom-call(bf16[4096,256]{1,0:T(8,128)(2,1)} %bitcast.5, bf16[4096,256]{1,0:T(8,128)(2,1)} %bitcast.6, bf16[256,1024]{1,0:T(8,128)(2,1)} %bitcast.7, s32[2,512]{1,0:T(2,128)} %bitcast.8, s32[16]{0:T(128)} %orders.1, s32[16]{0:T(128)} %dest.1), custom_call_target="tpu_custom_call" | custom-call | tf_op jit(solution)/shard_map/pallas_call | solution.py:262
  72.5 19.1 %shard_map.65 = f32[32,512]{1,0:T(8,128)} custom-call(f32[512,512]{1,0:T(8,128)} %shard_map.64.s_ref), custom_call_target="tpu_custom_call" | custom-call | tf_op jit(solution)/shard_map/pallas_call | solution.py:350

commit v4 on v3

--- a/solution.py
+++ b/solution.py
@@ -279,53 +279,75 @@
 
 
 def lane_of(x, k):
-    return jnp.broadcast_to(x[:, k:k + 1], x.shape)
+    return jnp.broadcast_to(x[:, k:k + 1], (8, 128))
 
 
 def sub_of(x, k):
     return jnp.broadcast_to(x[k:k + 1, :], x.shape)
 
 
-def panel(work, lo, p, lanes):
+def panel(work, lo, p, lanes, cols):
     wide = [lo + 128 * v for v in range(lanes)]
     top = lo + 8 * p
     rows = [work[pl.ds(top, 8), pl.ds(w, 128)] for w in wide]
     sub = lax.broadcasted_iota(jnp.int32, (8, 128), 0)
-    cols = [lane_of(rows[0], 8 * p + b) for b in range(8)]
+    if cols is None:
+        cols = [lane_of(rows[0], 8 * p + b) for b in range(8)]
+    ahead = None
+    inv, coef, urow = [], [], []
     scale = jnp.zeros((8, 128), jnp.float32)
-    inv, coef, urow = [], [], []
+    if p < 15:
+        nxt = work[pl.ds(top + 8, 8), pl.ds(lo, 128)]
+        side = [lane_of(nxt, 8 * p + b) for b in range(8)]
+        ahead = [lane_of(nxt, 8 * p + 8 + b) for b in range(8)]
     for k in range(8):
         r = lax.rsqrt(sub_of(cols[k], k))
+        d = r * r
         c = cols[k] * r
-        cs = {b: sub_of(c, b) for b in range(k + 1, 8)}
+        cs = {b: sub_of(cols[k], b) for b in range(k + 1, 8)}
         for b in range(k + 1, 8):
-            cols[b] = cols[b] - c * cs[b]
+            cols[b] = cols[b] - (cols[k] * cs[b]) * d
         u = [sub_of(x, k) * r for x in rows]
         cm = jnp.where(sub > k, c, 0.0)
         rows = [x - cm * y for x, y in zip(rows, u)]
         scale = jnp.where(sub == k, r, scale)
-        inv.append(r); coef.append(cs); urow.append(u)
-    for x, w in zip(rows, wide):
-        work[pl.ds(top, 8), pl.ds(w, 128)] = x * scale
+        inv.append(r)
+        coef.append({b: x * r for b, x in cs.items()})
+        urow.append(u)
+        if ahead is not None:
+            e = side[k] * r
+            for b in range(k + 1, 8):
+                side[b] = side[b] - e * coef[k][b]
+            ahead = [x - e * sub_of(e, b) for b, x in enumerate(ahead)]
+            side[k] = e
+    done = [x * scale for x in rows]
+    for x, w in zip(done, wide):
+        work[pl.ds(top, 8), pl.ds(w, 128)] = x
     for g in range(p + 1, 16):
         at = lo + 8 * g
         rest = [work[pl.ds(at, 8), pl.ds(w, 128)] for w in wide]
-        cols = [lane_of(rest[0], 8 * p + b) for b in range(8)]
+        if g == p + 1:
+            cs = side
+        else:
+            cs = [lane_of(rest[0], 8 * p + b) for b in range(8)]
+            for k in range(8):
+                cs[k] = cs[k] * inv[k]
+                for b in range(k + 1, 8):
+                    cs[b] = cs[b] - cs[k] * coef[k][b]
         for k in range(8):
-            c = cols[k] * inv[k]
-            for b in range(k + 1, 8):
-                cols[b] = cols[b] - c * coef[k][b]
-            rest = [x - c * y for x, y in zip(rest, urow[k])]
+            rest = [x - cs[k] * y for x, y in zip(rest, urow[k])]
         for x, w in zip(rest, wide):
             work[pl.ds(at, 8), pl.ds(w, 128)] = x
+    return ahead
 
 
 def factor(work, low, n):
     blocks = n // 128
     for j in range(blocks):
         lo = 128 * j
+        cols = None
         for p in range(16):
-            panel(work, lo, p, blocks - j)
+            cols = panel(work, lo, p, blocks - j, cols)
         tri = lax.broadcasted_iota(jnp.int32, (128, 128), 0) >= lax.broadcasted_iota(jnp.int32, (128, 128), 1)
         low[pl.ds(lo, 128), pl.ds(lo, 128)] = jnp.where(tri, work[pl.ds(lo, 128), pl.ds(lo, 128)].T, 0.0)
         for i in range(j + 1, blocks):

time: 91.7 us -> 87.7 us (0.956)
  Pallas kernels: 91.5 us -> 87.6 us
    pallas_call x1, Pallas kernels: 19.1 us -> 15.2 us  [chol_rows(): pl.pallas_call(chol_kernel, out_shape=jax.ShapeDtypeStruct((share, n), jn...]
where the time goes in v4:
time: 87.7 us; the launch traced here: 87.6 us
  Pallas kernels  87.6 us (100%)
    pallas_call x1, Pallas kernels, schur_block(): pl.pallas_call(pair_kernel, out_shape=jax.ShapeDtypeStruct((ORDER, ORDER)...  72.4 us
    pallas_call x1, Pallas kernels, chol_rows(): pl.pallas_call(chol_kernel, out_shape=jax.ShapeDtypeStruct((share, n), jn...  15.2 us

profile of v4, /device:TPU:1, one launch (start us, length us, event | category | flops | bytes accessed | tf_op | source)
XLA Modules:
  0.0 87.6 jit_solution(6947697911344910638)
XLA Ops:
  0.0 72.4 %shard_map.64.s_ref = f32[512,512]{1,0:T(8,128)} custom-call(bf16[4096,256]{1,0:T(8,128)(2,1)} %bitcast.5, bf16[4096,256]{1,0:T(8,128)(2,1)} %bitcast.6, bf16[256,1024]{1,0:T(8,128)(2,1)} %bitcast.7, s32[2,512]{1,0:T(2,128)} %bitcast.8, s32[16]{0:T(128)} %orders.1, s32[16]{0:T(128)} %dest.1), custom_call_target="tpu_custom_call" | custom-call | tf_op jit(solution)/shard_map/pallas_call | solution.py:262
  72.5 15.2 %shard_map.65 = f32[32,512]{1,0:T(8,128)} custom-call(f32[512,512]{1,0:T(8,128)} %shard_map.64.s_ref), custom_call_target="tpu_custom_call" | custom-call | tf_op jit(solution)/shard_map/pallas_call | solution.py:372

commit v5 on v4

--- a/solution.py
+++ b/solution.py
@@ -286,7 +286,7 @@
     return jnp.broadcast_to(x[k:k + 1, :], x.shape)
 
 
-def panel(work, lo, p, lanes, cols):
+def panel(work, lo, p, end, lanes, cols):
     wide = [lo + 128 * v for v in range(lanes)]
     top = lo + 8 * p
     rows = [work[pl.ds(top, 8), pl.ds(w, 128)] for w in wide]
@@ -296,7 +296,7 @@
     ahead = None
     inv, coef, urow = [], [], []
     scale = jnp.zeros((8, 128), jnp.float32)
-    if p < 15:
+    if p + 1 < end:
         nxt = work[pl.ds(top + 8, 8), pl.ds(lo, 128)]
         side = [lane_of(nxt, 8 * p + b) for b in range(8)]
         ahead = [lane_of(nxt, 8 * p + 8 + b) for b in range(8)]
@@ -323,7 +323,7 @@
     done = [x * scale for x in rows]
     for x, w in zip(done, wide):
         work[pl.ds(top, 8), pl.ds(w, 128)] = x
-    for g in range(p + 1, 16):
+    for g in range(p + 1, end):
         at = lo + 8 * g
         rest = [work[pl.ds(at, 8), pl.ds(w, 128)] for w in wide]
         if g == p + 1:
@@ -347,7 +347,12 @@
         lo = 128 * j
         cols = None
         for p in range(16):
-            cols = panel(work, lo, p, blocks - j, cols)
+            if p == 8:
+                left = work[pl.ds(lo, 64), pl.ds(lo, 128)].T[64:, :]
+                work[pl.ds(lo + 64, 64), pl.ds(lo, n - lo)] = work[pl.ds(lo + 64, 64), pl.ds(lo, n - lo)] - lax.dot_general(
+                    left, work[pl.ds(lo, 64), pl.ds(lo, n - lo)], (((1,), (0,)), ((), ())),
+                    preferred_element_type=jnp.float32, precision=lax.Precision.HIGHEST)
+            cols = panel(work, lo, p, 8 if p < 8 else 16, blocks - j, cols)
         tri = lax.broadcasted_iota(jnp.int32, (128, 128), 0) >= lax.broadcasted_iota(jnp.int32, (128, 128), 1)
         low[pl.ds(lo, 128), pl.ds(lo, 128)] = jnp.where(tri, work[pl.ds(lo, 128), pl.ds(lo, 128)].T, 0.0)
         for i in range(j + 1, blocks):

time: 87.7 us -> 85.5 us (0.975)
  Pallas kernels: 87.6 us -> 85.3 us
    pallas_call x1, Pallas kernels: 15.2 us -> 12.9 us  [chol_rows(): pl.pallas_call(chol_kernel, out_shape=jax.ShapeDtypeStruct((share, n), jn...]
where the time goes in v5:
time: 85.5 us; the launch traced here: 85.3 us
  Pallas kernels  85.3 us (100%)
    pallas_call x1, Pallas kernels, schur_block(): pl.pallas_call(pair_kernel, out_shape=jax.ShapeDtypeStruct((ORDER, ORDER)...  72.4 us
    pallas_call x1, Pallas kernels, chol_rows(): pl.pallas_call(chol_kernel, out_shape=jax.ShapeDtypeStruct((share, n), jn...  12.9 us

profile of v5, /device:TPU:1, one launch (start us, length us, event | category | flops | bytes accessed | tf_op | source)
XLA Modules:
  0.0 85.3 jit_solution(2716378467590455535)
XLA Ops:
  0.0 72.4 %shard_map.64.s_ref = f32[512,512]{1,0:T(8,128)} custom-call(bf16[4096,256]{1,0:T(8,128)(2,1)} %bitcast.5, bf16[4096,256]{1,0:T(8,128)(2,1)} %bitcast.6, bf16[256,1024]{1,0:T(8,128)(2,1)} %bitcast.7, s32[2,512]{1,0:T(2,128)} %bitcast.8, s32[16]{0:T(128)} %orders.1, s32[16]{0:T(128)} %dest.1), custom_call_target="tpu_custom_call" | custom-call | tf_op jit(solution)/shard_map/pallas_call | solution.py:262
  72.5 12.9 %shard_map.65 = f32[32,512]{1,0:T(8,128)} custom-call(f32[512,512]{1,0:T(8,128)} %shard_map.64.s_ref), custom_call_target="tpu_custom_call" | custom-call | tf_op jit(solution)/shard_map/pallas_call | solution.py:377

commit v6 on v5

--- a/solution.py
+++ b/solution.py
@@ -200,58 +200,67 @@
     col = jnp.where(low_part, 128 * a + lane, 128 * (3 - a) + lane - cut)
     order = orders[group]
     live = (row < order) & (col < order)
-    formed[...] = jnp.where(live, both[0] * both[1], 0.0) + jnp.where(row == col, 1.0, 0.0)
-
-    first = [send(formed, along.at[d - 1], x_sem, d - 1, {"blk": x_at(d)}) for d in (1, 2, 3)]
-    for copy in first:
+    value = jnp.where(live, both[0] * both[1], 0.0) + jnp.where(row == col, 1.0, 0.0)
+    for q in range(2):
+        formed[q] = value[8 * q:8 * q + 8, :]
+
+    first = [[send(formed.at[q], along.at[q, d - 1], x_sem, 3 * q + d - 1, {"blk": x_at(d)}) for d in (1, 2, 3)]
+             for q in range(2)]
+    for copy in first[0] + first[1]:
         copy.start()
-    have = [(group, formed[...])]
-    for d in (1, 2, 3):
-        first[d - 1].wait_recv()
-        have.append((x_at(4 - d), along[d - 1]))
-
-    def bound_for(to):
-        kept = jnp.zeros((16, FOLD), jnp.float32)
-        for source, value in have:
-            kept = jnp.where(dest[source] == to, value, kept)
-        return kept
-
-    second = []
-    for d in (2, 1, 3):
-        bound[d - 1] = bound_for(h_at(d))
-        copy = send(bound.at[d - 1], brought.at[d - 1], h_sem, d - 1, {"blk": h_at(d)})
-        copy.start()
-        second.append((d, copy))
-    here = bound_for(group)
-    for d, copy in second:
-        copy.wait_recv()
-        here = here + brought[d - 1]
-    pieces[me] = here
-
-    outs = [send(pieces.at[me], pieces.at[me], out_sem, 0, sibling)]
-    for n, (dy, dz) in enumerate(others):
-        yy, zz = chip_at(dy, dz)
-        outs.append(send(pieces.at[me], pieces.at[me], out_sem, 1 + n, at(yy, zz, k)))
-    for copy in outs:
-        copy.start()
+    second, here = [[], []], []
+    for q in range(2):
+        have = [(group, formed[q])]
+        for d in (1, 2, 3):
+            first[q][d - 1].wait_recv()
+            have.append((x_at(4 - d), along[q, d - 1]))
+
+        def bound_for(to):
+            kept = jnp.zeros((8, FOLD), jnp.float32)
+            for source, piece in have:
+                kept = jnp.where(dest[source] == to, piece, kept)
+            return kept
+
+        for d in (2, 1, 3):
+            bound[q, d - 1] = bound_for(h_at(d))
+            copy = send(bound.at[q, d - 1], brought.at[q, d - 1], h_sem, 3 * q + d - 1, {"blk": h_at(d)})
+            copy.start()
+            second[q].append(copy)
+        here.append(bound_for(group))
+
+    outs = [[], []]
+    for q in range(2):
+        for n, d in enumerate((2, 1, 3)):
+            second[q][n].wait_recv()
+            here[q] = here[q] + brought[q, d - 1]
+        pieces[q, me] = here[q]
+        for n, (dy, dz) in enumerate(others):
+            yy, zz = chip_at(dy, dz)
+            outs[q].append(send(pieces.at[q, me], pieces.at[q, me], out_sem, 15 * q + n, at(yy, zz, k)))
+        outs[q].append(send(pieces.at[q, me], pieces.at[q, me], out_sem, 15 * q + 7, sibling))
+        for copy in outs[q]:
+            copy.start()
     passed = []
-    for n, (dy, dz) in enumerate(others):
-        yy, zz = chip_at(4 - dy, dz)
-        source = 4 * yy + 2 * zz + k
-        outs[1 + n].wait_recv()
-        copy = send(pieces.at[source], pieces.at[source], out_sem, 8 + n, sibling)
-        copy.start()
-        passed.append(copy)
-    outs[0].wait_recv()
+    for q in range(2):
+        for n, (dy, dz) in enumerate(others):
+            yy, zz = chip_at(4 - dy, dz)
+            source = 4 * yy + 2 * zz + k
+            outs[q][n].wait_recv()
+            copy = send(pieces.at[q, source], pieces.at[q, source], out_sem, 15 * q + 8 + n, sibling)
+            copy.start()
+            passed.append(copy)
+    for q in range(2):
+        outs[q][7].wait_recv()
     for copy in passed:
         copy.wait_recv()
     for i in range(16):
         for row, col, lane, width in folded(i):
-            s_ref[row:row + 16, col:col + width] = pieces[i, :, lane:lane + width]
+            for q in range(2):
+                s_ref[row + 8 * q:row + 8 * q + 8, col:col + width] = pieces[q, i, :, lane:lane + width]
 
     own_copy.wait_send()
-    for copies in (z_copy, u_copy, w_copy, p_own, near[1], near[2], near[3], near[4], half_copy, *sums, first,
-                   [copy for _, copy in second], outs, passed):
+    for copies in (z_copy, u_copy, w_copy, p_own, near[1], near[2], near[3], near[4], half_copy, *sums, *first,
+                   *second, *outs, passed):
         for copy in copies:
             copy.wait_send()
 
@@ -269,10 +278,10 @@
             vm((2, 5, 512, 256), bf), vm((512, 2560), bf), vm((5, 512, RANK), bf),
             vm((512, RANK), f32), vm((2, ORDER, RANK), bf), vm((2, ORDER, 512), bf),
             vm((2, 2, 8, 16, FOLD), f32), vm((2, 8, 16, FOLD), f32), vm((2, 8, 16, FOLD), f32),
-            vm((2, 7, 16, FOLD), f32), vm((16, FOLD), f32), vm((3, 16, FOLD), f32), vm((3, 16, FOLD), f32),
-            vm((3, 16, FOLD), f32), vm((16, 16, FOLD), f32),
+            vm((2, 7, 16, FOLD), f32), vm((2, 8, FOLD), f32), vm((2, 3, 8, FOLD), f32), vm((2, 3, 8, FOLD), f32),
+            vm((2, 3, 8, FOLD), f32), vm((2, 16, 8, FOLD), f32),
             dma((10,)), dma((2, 1)), dma((2, 4 * CHUNKS)), dma((2, 4 * CHUNKS)), dma((2, 16)),
-            dma((2, 3)), dma((2, 3)), dma((2, 15)),
+            dma((2, 6)), dma((2, 6)), dma((2, 30)),
         ],
         compiler_params=pltpu.CompilerParams(collective_id=0, has_side_effects=True),
     )(x, y, v, index, orders, dest)

time: 85.5 us -> 84.9 us (level)
  no operation moved by 1% of the time
where the time goes in v6:
time: 84.9 us; the launch traced here: 84.8 us
  Pallas kernels  84.8 us (100%)
    pallas_call x1, Pallas kernels, schur_block(): pl.pallas_call(pair_kernel, out_shape=jax.ShapeDtypeStruct((ORDER, ORDER)...  71.9 us
    pallas_call x1, Pallas kernels, chol_rows(): pl.pallas_call(chol_kernel, out_shape=jax.ShapeDtypeStruct((share, n), jn...  12.9 us

profile of v6, /device:TPU:1, one launch (start us, length us, event | category | flops | bytes accessed | tf_op | source)
XLA Modules:
  0.0 84.8 jit_solution(16104128900296638049)
XLA Ops:
  0.0 71.9 %shard_map.64.s_ref = f32[512,512]{1,0:T(8,128)} custom-call(bf16[4096,256]{1,0:T(8,128)(2,1)} %bitcast.5, bf16[4096,256]{1,0:T(8,128)(2,1)} %bitcast.6, bf16[256,1024]{1,0:T(8,128)(2,1)} %bitcast.7, s32[2,512]{1,0:T(2,128)} %bitcast.8, s32[16]{0:T(128)} %orders.1, s32[16]{0:T(128)} %dest.1), custom_call_target="tpu_custom_call" | custom-call | tf_op jit(solution)/shard_map/pallas_call | solution.py:271
  71.9 12.9 %shard_map.65 = f32[32,512]{1,0:T(8,128)} custom-call(f32[512,512]{1,0:T(8,128)} %shard_map.64.s_ref), custom_call_target="tpu_custom_call" | custom-call | tf_op jit(solution)/shard_map/pallas_call | solution.py:386
